TPU v7x, 256 devices: a whole 4x4x8 slice. The times are simulated.
256 devices in a mesh: gx: 4 (over x), gy: 4 (over y), gz: 16 (over z, core).
Axes of the slice: x: 4, y: 4, z: 8, core: 2. Of those that a mesh axis runs over, the one named last changes fastest.
Arguments:
- embeds: bfloat16 [2048, 128, 2048], P(('gx', 'gy', 'gz')), may hold values from -6 to 6
- dest_device: int32 [2048], P(('gx', 'gy', 'gz')), may hold values from 0 to 255, as said below
- shuffle_key: int32 [2048], P(('gx', 'gy', 'gz')), may hold values from 0 to 2047, each once
- lengths: int32 [64], replicated, may hold values from 1 to 4096
- gain: float32 [2048], replicated, may hold values from 0.1 to 1.9
Outputs:
- packed: bfloat16 [4096, 128, 2048], P(('gx', 'gy', 'gz'))
Inputs may be any that keep to these rules, and one draw needn't show every extreme that they name: `dest_device`: device numbers are ((gx * 4) + gy) * 16 + gz. A device receives at most 16 tiles, and in every draw some devices receive exactly 16. The 16 devices sharing gx and gy send at most one tile to any one device and exactly 8 tiles to the devices of each gz index. Of one device's tiles at most 1 go to devices of one gz index, and some device reaches that.
All inputs are finite; a program needn't handle non-finite values.
Results may differ from a plain program's by a relative error of at most 0.001.
Values may be sent and summed in bfloat16 or wider, within the bound.
A program may use at most 128 MiB of HBM per device.

v0:
```python
import functools

import jax
import jax.numpy as jnp
from jax import lax
from jax.experimental import pallas as pl
from jax.experimental.pallas import tpu as pltpu
from jax.sharding import PartitionSpec as P

MESH = pl.DeviceIdType.MESH
TILES_SEQ = 32
ROWS = 16
AHEAD = 2
PIECES = (640, 512, 512, 384)


def exchange(
    sizes,
    embeds,
    dest_hbm,
    key_hbm,
    lengths_hbm,
    gain_hbm,
    ranked,
    held,
    gain,
    fresh,
    send1,
    recv1,
    stage1,
    send2,
    recv2,
    stage2,
    note1,
    noted1,
    note2,
    noted2,
    dest,
    key,
    lengths,
    read1,
    read2,
    tile_of,
    source_of,
    place_of,
    slot_of,
    load_sem,
    send1_sem,
    recv1_sem,
    send2_sem,
    recv2_sem,
    note_sem,
    read_sem,
):
    nx, ny, nz = sizes
    groups = nx * ny
    tiles, tile_rows, width = embeds.shape
    chunks = tile_rows // ROWS
    last = chunks - 1
    gx, gy, gz = lax.axis_index("gx"), lax.axis_index("gy"), lax.axis_index("gz")
    group = gx * ny + gy
    first_tile = (group * nz + gz) * tiles

    def z_peer(step):
        half = step // 2
        away = jnp.where(lax.rem(step, 2) == 0, nz // 2 - half, nz // 2 + half)
        return lax.rem(gz + away, nz)

    away_xy = sorted(
        ((dx, dy) for dx in range(nx) for dy in range(ny) if dx or dy),
        key=lambda d: -min(d[0], nx - d[0]) - min(d[1], ny - d[1]),
    )

    def xy_peer(step):
        dx, dy = away_xy[step - 1]
        return lax.rem(gx + dx, nx), lax.rem(gy + dy, ny)

    barrier = pltpu.get_barrier_semaphore()

    @pl.loop(1, nz)
    def _(step):
        pl.semaphore_signal(
            barrier, inc=1, device_id={"gz": z_peer(step)}, device_id_type=MESH
        )

    for step in range(1, groups):
        x, y = xy_peer(step)
        pl.semaphore_signal(
            barrier, inc=1, device_id={"gx": x, "gy": y}, device_id_type=MESH
        )

    first_rows = pl.ds(0, ROWS)
    other_rows = pl.ds(ROWS, tile_rows - ROWS)
    loads = [
        pltpu.make_async_copy(src, dst, load_sem.at[i])
        for i, (src, dst) in enumerate(
            (
                (dest_hbm, dest),
                (key_hbm, key),
                (lengths_hbm, lengths),
                (gain_hbm, gain),
                (embeds.at[:, first_rows], held.at[:, first_rows]),
                (embeds.at[:, other_rows], held.at[:, other_rows]),
            )
        )
    ]
    for load in loads:
        load.start()

    stage1[nz] = jnp.zeros(stage1.shape[1:], stage1.dtype)
    lane = lax.broadcasted_iota(jnp.int32, (1, 128), 1)
    row = lax.broadcasted_iota(jnp.int32, (ROWS, 1), 0)
    for load in loads[:4]:
        load.wait()

    @pl.loop(0, nz)
    def _(slot):
        tile = jnp.int32(-1)
        home = jnp.int32(-1)
        rank_key = jnp.int32(-1)
        for t in range(tiles):
            here = lax.rem(dest[t], nz) == slot
            tile = jnp.where(here, t, tile)
            home = jnp.where(here, lax.div(dest[t], nz), home)
            rank_key = jnp.where(here, key[t], rank_key)
        tile_of[slot] = jnp.maximum(tile, 0)
        note1[slot] = jnp.where(lane == 0, home, rank_key)

    noted1[gz] = note1[gz]

    limit = lengths[first_tile // TILES_SEQ]
    first_position = lax.rem(first_tile, TILES_SEQ) * tile_rows

    def wait_bytes(ref, count, sem):
        part = ref.at[pl.ds(0, count)]
        pltpu.make_async_copy(part, part, sem).wait()

    def whole(chunk):
        return chunk, chunk, pl.ds(0, width)

    def piece(p):
        return last, last + p, pl.ds(sum(PIECES[:p]), PIECES[p])

    def z_copy(part, step):
        chunk, sem, columns = part
        peer = z_peer(step)
        return pltpu.make_async_remote_copy(
            src_ref=send1.at[chunk, peer, :, columns],
            dst_ref=recv1.at[chunk, gz, :, columns],
            send_sem=send1_sem.at[sem],
            recv_sem=recv1_sem.at[sem],
            device_id={"gz": peer},
            device_id_type=MESH,
        )

    def xy_copy(part, step):
        chunk, sem, columns = part
        x, y = xy_peer(step)
        return pltpu.make_async_remote_copy(
            src_ref=send2.at[chunk, x * ny + y, :, columns],
            dst_ref=recv2.at[chunk, group, :, columns],
            send_sem=send2_sem.at[sem],
            recv_sem=recv2_sem.at[sem],
            device_id={"gx": x, "gy": y},
            device_id_type=MESH,
        )

    def make_chunk(chunk):
        start = pl.multiple_of(chunk * ROWS, ROWS)
        for t in range(tiles):
            values = held[t, pl.ds(start, ROWS), :].astype(jnp.float32)
            meansq = jnp.mean(values * values, axis=-1, keepdims=True)
            scaled = values * lax.rsqrt(jnp.maximum(meansq, 0.25)) * gain[...]
            position = first_position + t * tile_rows + start + row
            fresh[t] = jnp.where(position < limit, scaled, 0.0).astype(jnp.bfloat16)
        for step in range(1, nz):
            peer = z_peer(step)
            send1[chunk, peer] = fresh[tile_of[peer]]
        recv1[chunk, gz] = fresh[tile_of[gz]]

    def send_part(part):
        for step in range(1, nz):
            z_copy(part, step).start()

    def regroup(part):
        chunk, sem, columns = part
        wait_bytes(recv1.at[chunk, :, :, columns], nz - 1, recv1_sem.at[sem])
        for slot in range(nz):
            stage1[slot, :, columns] = recv1[chunk, slot, :, columns]
        for step in range(1, groups):
            x, y = xy_peer(step)
            target = x * ny + y
            send2[chunk, target, :, columns] = stage1[source_of[target], :, columns]
        recv2[chunk, group, :, columns] = stage1[source_of[group], :, columns]

        for step in range(1, groups):
            xy_copy(part, step).start()

    def finish(part):
        chunk, sem, columns = part
        wait_bytes(recv2.at[chunk, :, :, columns], groups - 1, recv2_sem.at[sem])
        for slot in range(groups):
            stage2[slot, :, columns] = recv2[chunk, slot, :, columns]
        start = pl.multiple_of(chunk * ROWS, ROWS)
        for place in range(groups):
            ranked[place, pl.ds(start, ROWS), columns] = stage2[
                slot_of[place], :, columns
            ]

    loads[4].wait()
    make_chunk(0)
    pl.semaphore_wait(barrier, nz + groups - 2)
    send_part(whole(0))

    def note1_copy(step):
        peer = z_peer(step)
        return pltpu.make_async_remote_copy(
            src_ref=note1.at[peer],
            dst_ref=noted1.at[gz],
            send_sem=note_sem.at[0],
            recv_sem=note_sem.at[1],
            device_id={"gz": peer},
            device_id_type=MESH,
        )

    def note2_copy(step):
        x, y = xy_peer(step)
        return pltpu.make_async_remote_copy(
            src_ref=note2.at[x * ny + y],
            dst_ref=noted2.at[group],
            send_sem=note_sem.at[2],
            recv_sem=note_sem.at[3],
            device_id={"gx": x, "gy": y},
            device_id_type=MESH,
        )

    @pl.loop(1, nz)
    def _(step):
        note1_copy(step).start()

    loads[5].wait()

    @pl.loop(1, AHEAD)
    def _(chunk):
        make_chunk(chunk)
        send_part(whole(chunk))

    wait_bytes(noted1, nz - 1, note_sem.at[1])
    read = pltpu.make_async_copy(noted1, read1, read_sem.at[0])
    read.start()
    read.wait()

    @pl.loop(0, groups)
    def _(target):
        source = jnp.int32(nz)
        rank_key = jnp.int32(-1)
        for s in range(nz):
            here = read1[s, 0, 0] == target
            source = jnp.where(here, s, source)
            rank_key = jnp.where(here, read1[s, 0, 1], rank_key)
        source_of[target] = source
        note2[target] = jnp.full((1, 128), rank_key, jnp.int32)

    noted2[group] = note2[group]

    for step in range(1, groups):
        note2_copy(step).start()

    make_chunk(AHEAD)
    send_part(whole(AHEAD))
    regroup(whole(0))

    wait_bytes(noted2, groups - 1, note_sem.at[3])
    read = pltpu.make_async_copy(noted2, read2, read_sem.at[1])
    read.start()
    read.wait()

    @pl.loop(0, groups)
    def _(slot):
        mine = read2[slot, 0, 0]
        place = jnp.int32(0)
        for other in range(groups):
            theirs = read2[other, 0, 0]
            before = jnp.where(
                mine >= 0,
                (theirs >= 0) & (theirs < mine),
                (theirs >= 0) | (other < slot),
            )
            place = place + before.astype(jnp.int32)
        place_of[slot] = place

    @pl.loop(0, groups)
    def _(place):
        found = jnp.int32(0)
        for slot in range(groups):
            found = jnp.where(place_of[slot] == place, slot, found)
        slot_of[place] = found

    @pl.loop(1, last)
    def _(chunk):
        @pl.when(chunk + AHEAD < last)
        def _():
            make_chunk(chunk + AHEAD)
            send_part(whole(chunk + AHEAD))

        @pl.when(chunk + AHEAD == last)
        def _():
            make_chunk(last)
            for p in range(len(PIECES)):
                send_part(piece(p))

        regroup(whole(chunk))
        finish(whole(chunk - 1))

    regroup(piece(0))
    finish(whole(last - 1))
    for p in range(1, len(PIECES)):
        regroup(piece(p))
        finish(piece(p - 1))
    finish(piece(len(PIECES) - 1))

    wait_bytes(note1, nz - 1, note_sem.at[0])
    wait_bytes(note2, groups - 1, note_sem.at[2])

    @pl.loop(0, last)
    def _(chunk):
        wait_bytes(send1.at[chunk], nz - 1, send1_sem.at[chunk])
        wait_bytes(send2.at[chunk], groups - 1, send2_sem.at[chunk])

    for p in range(len(PIECES)):
        chunk, sem, columns = piece(p)
        wait_bytes(send1.at[chunk, :, :, columns], nz - 1, send1_sem.at[sem])
        wait_bytes(send2.at[chunk, :, :, columns], groups - 1, send2_sem.at[sem])


def solution(mesh):
    sizes = (mesh.shape["gx"], mesh.shape["gy"], mesh.shape["gz"])
    groups, nz = sizes[0] * sizes[1], sizes[2]

    def shards(embeds, dest_device, shuffle_key, lengths, gain):
        tiles, tile_rows, width = embeds.shape
        chunks = tile_rows // ROWS
        parts = chunks - 1 + len(PIECES)
        any_space = pl.BlockSpec(memory_space=pl.ANY)
        rows = lambda *lead: pltpu.VMEM((*lead, ROWS, width), jnp.bfloat16)
        notes = lambda space, count: space((count, 1, 128), jnp.int32)
        return pl.pallas_call(
            functools.partial(exchange, sizes),
            out_shape=pltpu.VMEM((groups, tile_rows, width), jnp.bfloat16),
            in_specs=[any_space] * 5,
            out_specs=pl.BlockSpec(memory_space=pltpu.VMEM),
            scratch_shapes=[
                pltpu.VMEM((tiles, tile_rows, width), jnp.bfloat16),
                pltpu.VMEM((1, width), jnp.float32),
                rows(tiles),
                rows(chunks, nz),
                rows(chunks, nz),
                rows(nz + 1),
                rows(chunks, groups),
                rows(chunks, groups),
                rows(groups),
                notes(pltpu.VMEM, nz),
                notes(pltpu.VMEM, nz),
                notes(pltpu.VMEM, groups),
                notes(pltpu.VMEM, groups),
                pltpu.SMEM(dest_device.shape, jnp.int32),
                pltpu.SMEM(shuffle_key.shape, jnp.int32),
                pltpu.SMEM(lengths.shape, jnp.int32),
                notes(pltpu.SMEM, nz),
                notes(pltpu.SMEM, groups),
                pltpu.SMEM((nz,), jnp.int32),
                pltpu.SMEM((groups,), jnp.int32),
                pltpu.SMEM((groups,), jnp.int32),
                pltpu.SMEM((groups,), jnp.int32),
                pltpu.SemaphoreType.DMA((6,)),
                pltpu.SemaphoreType.DMA((parts,)),
                pltpu.SemaphoreType.DMA((parts,)),
                pltpu.SemaphoreType.DMA((parts,)),
                pltpu.SemaphoreType.DMA((parts,)),
                pltpu.SemaphoreType.DMA((4,)),
                pltpu.SemaphoreType.DMA((2,)),
            ],
            compiler_params=pltpu.CompilerParams(
                collective_id=0, has_side_effects=True, vmem_limit_bytes=53 * 2**20
            ),
            name="exchange",
        )(embeds, dest_device, shuffle_key, lengths, gain.reshape(1, width))

    return jax.shard_map(
        shards,
        mesh=mesh,
        in_specs=(
            P(("gx", "gy", "gz"), None, None),
            P(("gx", "gy", "gz")),
            P(("gx", "gy", "gz")),
            P(),
            P(),
        ),
        out_specs=P(("gx", "gy", "gz"), None, None),
        check_vma=False,
    )
```

profile of v0, /device:TPU:32, one launch (start us, length us, event | category | flops | bytes accessed | tf_op | source)
XLA Modules:
  0.0 200.1 jit_solution(4872390476141539729)
XLA Ops:
  0.0 196.7 %exchange.1 = bf16[16,128,2048]{2,1,0:T(8,128)(2,1)S(1)} custom-call(bf16[8,128,2048]{2,1,0:T(8,128)(2,1)} %embeds.1, s32[8]{0:T(128)} %dest_hbm.1, s32[8]{0:T(128)} %key_hbm.1, s32[64]{0:T(128)} %lengths_hbm.1, f32[1,2048]{1,0:T(1,128)} %bitcast.1), custom_call_target="tpu_custom_call" | custom-call | tf_op jit(solution)/shard_map/exchange/pallas_call | solution.py:347
  196.7 3.4 %copy.7 = bf16[16,128,2048]{2,1,0:T(8,128)(2,1)} copy(bf16[16,128,2048]{2,1,0:T(8,128)(2,1)S(1)} %exchange.1) | data formatting | bytes 16777216
where the time goes:
time: 201 us; the launch traced here: 200 us
  Pallas kernels  197 us (98%)
  local copies, waits for them, and re-layouts  3.4 us (2%)
    pallas_call x1, Pallas kernels, shards(): pl.pallas_call(functools.partial(exchange, sizes), out_shape=pltpu.VMEM((...  197 us

commit v1 on v0

--- a/solution.py
+++ b/solution.py
@@ -11,6 +11,7 @@
 TILES_SEQ = 32
 ROWS = 16
 AHEAD = 2
+CORES = 2
 PIECES = (640, 512, 512, 384)
 
 
@@ -141,9 +142,26 @@
     def piece(p):
         return last, last + p, pl.ds(sum(PIECES[:p]), PIECES[p])
 
-    def z_copy(part, step):
+    def last_peers():
+        def order(me):
+            def rank(peer):
+                chip = peer // CORES
+                away = abs(chip - me // CORES)
+                return chip > 0, -min(away, nz // CORES - away), peer
+
+            return sorted((p for p in range(nz) if p != me), key=rank)
+
+        orders = [order(me) for me in range(nz)]
+        peers = []
+        for k in range(nz - 1):
+            peer = jnp.int32(orders[0][k])
+            for me in range(1, nz):
+                peer = jnp.where(gz == me, orders[me][k], peer)
+            peers.append(peer)
+        return peers
+
+    def z_copy(part, peer):
         chunk, sem, columns = part
-        peer = z_peer(step)
         return pltpu.make_async_remote_copy(
             src_ref=send1.at[chunk, peer, :, columns],
             dst_ref=recv1.at[chunk, gz, :, columns],
@@ -180,7 +198,7 @@
 
     def send_part(part):
         for step in range(1, nz):
-            z_copy(part, step).start()
+            z_copy(part, z_peer(step)).start()
 
     def regroup(part):
         chunk, sem, columns = part
@@ -306,8 +324,10 @@
         @pl.when(chunk + AHEAD == last)
         def _():
             make_chunk(last)
+            peers = last_peers()
             for p in range(len(PIECES)):
-                send_part(piece(p))
+                for peer in peers:
+                    z_copy(piece(p), peer).start()
 
         regroup(whole(chunk))
         finish(whole(chunk - 1))

time: 201 us -> 201 us (level)
  no operation moved by 1% of the time
where the time goes in v1:
time: 201 us
  Pallas kernels  197 us (98%)
  local copies, waits for them, and re-layouts  3.4 us (2%)
    pallas_call x1, Pallas kernels, shards(): pl.pallas_call(functools.partial(exchange, sizes), out_shape=pltpu.VMEM((...  197 us

profile of v1, /device:TPU:32, one launch (start us, length us, event | category | flops | bytes accessed | tf_op | source)
XLA Modules:
  0.0 200.5 jit_solution(17359226018668598861)
XLA Ops:
  0.0 197.1 %exchange.1 = bf16[16,128,2048]{2,1,0:T(8,128)(2,1)S(1)} custom-call(bf16[8,128,2048]{2,1,0:T(8,128)(2,1)} %embeds.1, s32[8]{0:T(128)} %dest_hbm.1, s32[8]{0:T(128)} %key_hbm.1, s32[64]{0:T(128)} %lengths_hbm.1, f32[1,2048]{1,0:T(1,128)} %bitcast.1), custom_call_target="tpu_custom_call" | custom-call | tf_op jit(solution)/shard_map/exchange/pallas_call | solution.py:367
  197.1 3.4 %copy.7 = bf16[16,128,2048]{2,1,0:T(8,128)(2,1)} copy(bf16[16,128,2048]{2,1,0:T(8,128)(2,1)S(1)} %exchange.1) | data formatting | bytes 16777216

commit v2 on v1

--- a/solution.py
+++ b/solution.py
@@ -12,7 +12,7 @@
 ROWS = 16
 AHEAD = 2
 CORES = 2
-PIECES = (640, 512, 512, 384)
+PIECES = (640, 512, 512, 256, 128)
 
 
 def exchange(
@@ -336,8 +336,8 @@
     finish(whole(last - 1))
     for p in range(1, len(PIECES)):
         regroup(piece(p))
-        finish(piece(p - 1))
-    finish(piece(len(PIECES) - 1))
+    for p in range(len(PIECES)):
+        finish(piece(p))
 
     wait_bytes(note1, nz - 1, note_sem.at[0])
     wait_bytes(note2, groups - 1, note_sem.at[2])

time: 201 us -> 201 us (level)
  no operation moved by 1% of the time
where the time goes in v2:
time: 201 us; the launch traced here: 200 us
  Pallas kernels  197 us (98%)
  local copies, waits for them, and re-layouts  3.4 us (2%)
    pallas_call x1, Pallas kernels, shards(): pl.pallas_call(functools.partial(exchange, sizes), out_shape=pltpu.VMEM((...  197 us

profile of v2, /device:TPU:32, one launch (start us, length us, event | category | flops | bytes accessed | tf_op | source)
XLA Modules:
  0.0 200.1 jit_solution(10191847430904513075)
XLA Ops:
  0.0 196.7 %exchange.1 = bf16[16,128,2048]{2,1,0:T(8,128)(2,1)S(1)} custom-call(bf16[8,128,2048]{2,1,0:T(8,128)(2,1)} %embeds.1, s32[8]{0:T(128)} %dest_hbm.1, s32[8]{0:T(128)} %key_hbm.1, s32[64]{0:T(128)} %lengths_hbm.1, f32[1,2048]{1,0:T(1,128)} %bitcast.1), custom_call_target="tpu_custom_call" | custom-call | tf_op jit(solution)/shard_map/exchange/pallas_call | solution.py:367
  196.7 3.4 %copy.7 = bf16[16,128,2048]{2,1,0:T(8,128)(2,1)} copy(bf16[16,128,2048]{2,1,0:T(8,128)(2,1)S(1)} %exchange.1) | data formatting | bytes 16777216

commit v3 on v1

--- a/solution.py
+++ b/solution.py
@@ -12,6 +12,7 @@
 ROWS = 16
 AHEAD = 2
 CORES = 2
+STORES = 4
 PIECES = (640, 512, 512, 384)
 
 
@@ -353,6 +354,20 @@
         wait_bytes(send2.at[chunk, :, :, columns], groups - 1, send2_sem.at[sem])
 
 
+def store(ranked, packed, sem):
+    each = packed.shape[0] // STORES
+    copies = []
+    for i in range(STORES):
+        part = pl.ds(i * each, each)
+        copies.append(
+            pltpu.make_async_copy(ranked.at[part], packed.at[part], sem.at[i])
+        )
+    for copy in copies:
+        copy.start()
+    for copy in copies:
+        copy.wait()
+
+
 def solution(mesh):
     sizes = (mesh.shape["gx"], mesh.shape["gy"], mesh.shape["gz"])
     groups, nz = sizes[0] * sizes[1], sizes[2]
@@ -364,7 +379,7 @@
         any_space = pl.BlockSpec(memory_space=pl.ANY)
         rows = lambda *lead: pltpu.VMEM((*lead, ROWS, width), jnp.bfloat16)
         notes = lambda space, count: space((count, 1, 128), jnp.int32)
-        return pl.pallas_call(
+        ranked = pl.pallas_call(
             functools.partial(exchange, sizes),
             out_shape=pltpu.VMEM((groups, tile_rows, width), jnp.bfloat16),
             in_specs=[any_space] * 5,
@@ -405,6 +420,15 @@
             ),
             name="exchange",
         )(embeds, dest_device, shuffle_key, lengths, gain.reshape(1, width))
+        return pl.pallas_call(
+            store,
+            out_shape=jax.ShapeDtypeStruct((groups, tile_rows, width), jnp.bfloat16),
+            in_specs=[pl.BlockSpec(memory_space=pltpu.VMEM)],
+            out_specs=any_space,
+            scratch_shapes=[pltpu.SemaphoreType.DMA((STORES,))],
+            compiler_params=pltpu.CompilerParams(vmem_limit_bytes=2**20),
+            name="store",
+        )(ranked)
 
     return jax.shard_map(
         shards,

time: 201 us -> 201 us (level)
  local copies, waits for them, and re-layouts: 3.4 us -> 0 us
  Pallas kernels: 197 us -> 200 us
    unnamed x1 -> x0, local copies, waits for them, and re-layouts: 3.4 us -> none
    pallas_call x0 -> x1, Pallas kernels: none -> 3.37 us  [shards(): pl.pallas_call(store, out_shape=jax.ShapeDtypeStruct((groups, tile_rows,...]
where the time goes in v3:
time: 201 us; the launch traced here: 200 us
  Pallas kernels  200 us (100%)
    pallas_call x1, Pallas kernels, shards(): pl.pallas_call(functools.partial(exchange, sizes), out_shape=pltpu.VMEM((...  197 us

profile of v3, /device:TPU:32, one launch (start us, length us, event | category | flops | bytes accessed | tf_op | source)
XLA Modules:
  0.0 200.5 jit_solution(9654043984538822908)
XLA Ops:
  0.0 197.1 %exchange.1.ranked = bf16[16,128,2048]{2,1,0:T(8,128)(2,1)S(1)} custom-call(bf16[8,128,2048]{2,1,0:T(8,128)(2,1)} %embeds.1, s32[8]{0:T(128)} %dest_hbm.1, s32[8]{0:T(128)} %key_hbm.1, s32[64]{0:T(128)} %lengths_hbm.1, f32[1,2048]{1,0:T(1,128)} %bitcast.1), custom_call_target="tpu_custom_call" | custom-call | tf_op jit(solution)/shard_map/exchange/pallas_call | solution.py:382
  197.1 3.4 %store.1 = bf16[16,128,2048]{2,1,0:T(8,128)(2,1)} custom-call(bf16[16,128,2048]{2,1,0:T(8,128)(2,1)S(1)} %exchange.1.ranked), custom_call_target="tpu_custom_call" | custom-call | tf_op jit(solution)/shard_map/store/pallas_call | solution.py:423
